TPU v7x, 32 devices: a whole 2x2x4 slice. The times are simulated.
32 devices in a mesh: dp: 8 (over y, x, core), mp: 4 (over z).
Axes of the slice: x: 2, y: 2, z: 4, core: 2. Of those that a mesh axis runs over, the one named last changes fastest.
Arguments:
- states: bfloat16 [128, 80, 768], P('dp'), may hold values from -6 to 6
- hist_len: int32 [128], P('dp'), may hold values from 1 to 20
- norm_gain: float32 [768], replicated, may hold values from 0.5 to 1.5
- qkv_weight: bfloat16 [768, 3, 12, 64], P(None, None, 'mp'), may hold values from -1 to 1
- output_weight: bfloat16 [12, 64, 768], P('mp'), may hold values from -0.21875 to 0.21875
- cotangent: bfloat16 [128, 80, 768], P('dp'), may hold values from -6 to 6
Outputs:
- attended: bfloat16 [128, 80, 768], P('dp')
- grad_states: bfloat16 [128, 80, 768], P('dp')
- grad_qkv: float32 [768, 3, 12, 64], P('dp', None, 'mp')
- output_weight_gradient: float32 [12, 64, 768], P('mp', None, 'dp')
- grad_gain: float32 [768], P('dp')
All inputs are finite; a program needn't handle non-finite values.
Results may differ from a plain program's by a relative error of at most 0.012.
Values may be sent and summed in bfloat16 or wider, within the bound.
A program may use at most 128 MiB of HBM per device.

v0:
```python
import jax
import jax.numpy as jnp
from jax import lax
from jax.sharding import PartitionSpec as P

LEVELS = 4


def body(states, hist_len, norm_gain, qkv_weight, output_weight, cotangent):
    wide_states = states.astype(jnp.float32)
    inv_rms = lax.rsqrt(jnp.mean(wide_states * wide_states, axis=-1, keepdims=True) + 1e-06)
    unit = wide_states * inv_rms
    normed = (unit * norm_gain).astype(jnp.bfloat16)
    proj = jnp.einsum(
        "bsd,dchk->bschk", normed, qkv_weight, preferred_element_type=jnp.float32
    ).astype(jnp.bfloat16)
    queries = proj[:, :, 0]
    key_rows = proj[:, :, 1]
    value_rows = proj[:, :, 2]
    positions = jnp.arange(states.shape[1], dtype=jnp.int32)
    keep_mask = positions[None, :] < LEVELS * hist_len[:, None]
    scores = jnp.einsum("bqhk,bphk->bhqp", queries, key_rows, preferred_element_type=jnp.float32)
    masked = jnp.where(keep_mask[:, None, None, :], scores, -1e30)
    row_top = jnp.max(masked, axis=-1, keepdims=True)
    exp_scores = jnp.exp(masked - row_top)
    attn_prob = exp_scores / jnp.sum(exp_scores, axis=-1, keepdims=True)
    prob_bf = attn_prob.astype(jnp.bfloat16)
    attended_context = jnp.einsum(
        "bhqp,bphk->bqhk", prob_bf, value_rows, preferred_element_type=jnp.float32
    ).astype(jnp.bfloat16)
    partial_mix = jnp.einsum(
        "zagm,gms->zas", attended_context, output_weight, preferred_element_type=jnp.float32
    )
    mixed_total_sum = lax.psum(partial_mix.astype(jnp.bfloat16), "mp").astype(jnp.float32)
    attended = (wide_states + mixed_total_sum).astype(jnp.bfloat16)
    masked_cotangent = jnp.where(keep_mask[:, :, None], cotangent, jnp.zeros_like(cotangent))
    local_output = jnp.einsum(
        "wmep,wmx->epx", attended_context, masked_cotangent, preferred_element_type=jnp.float32
    )
    context_gradient = jnp.einsum(
        "uxy,wgy->uxwg", masked_cotangent, output_weight, preferred_element_type=jnp.float32
    ).astype(jnp.bfloat16)
    grad_prob = jnp.einsum(
        "bqhk,bphk->bhqp", context_gradient, value_rows, preferred_element_type=jnp.float32
    )
    row_delta = jnp.sum(attn_prob * grad_prob, axis=-1, keepdims=True)
    grad_score = (attn_prob * (grad_prob - row_delta)).astype(jnp.bfloat16)
    grad_query = jnp.einsum(
        "bhqp,bphk->bqhk", grad_score, key_rows, preferred_element_type=jnp.float32
    )
    grad_key = jnp.einsum(
        "bhqp,bqhk->bphk", grad_score, queries, preferred_element_type=jnp.float32
    )
    grad_value = jnp.einsum(
        "bhqp,bqhk->bphk", prob_bf, context_gradient, preferred_element_type=jnp.float32
    )
    grad_proj = jnp.stack([grad_query, grad_key, grad_value], axis=2).astype(jnp.bfloat16)
    local_qkv = jnp.einsum("bsd,bschk->dchk", normed, grad_proj, preferred_element_type=jnp.float32)
    partial_normed = jnp.einsum(
        "bschk,dchk->bsd", grad_proj, qkv_weight, preferred_element_type=jnp.float32
    )
    wide_cot = masked_cotangent.astype(jnp.float32)
    grad_normed = lax.psum(partial_normed, "mp")
    local_gain = jnp.sum(grad_normed * unit, axis=(0, 1))
    unit_grad = grad_normed * norm_gain
    row_corr = jnp.mean(unit_grad * unit, axis=-1, keepdims=True)
    grad_states = (wide_cot + inv_rms * (unit_grad - unit * row_corr)).astype(jnp.bfloat16)
    grad_qkv, output_weight_gradient, grad_gain = (
        lax.psum_scatter(local_qkv, "dp", scatter_dimension=0, tiled=True),
        lax.psum_scatter(local_output, "dp", scatter_dimension=2, tiled=True),
        lax.psum_scatter(local_gain, "dp", scatter_dimension=0, tiled=True),
    )
    return (attended, grad_states, grad_qkv, output_weight_gradient, grad_gain)


def solution(mesh):
    placed = (
        P("dp", None, None),
        P("dp"),
        P(),
        P(None, None, "mp", None),
        P("mp", None, None),
        P("dp", None, None),
    )
    return jax.shard_map(
        body,
        mesh=mesh,
        in_specs=placed,
        out_specs=(
            P("dp", None, None),
            P("dp", None, None),
            P("dp", None, "mp", None),
            P("mp", None, "dp"),
            P("dp"),
        ),
        check_vma=False,
    )
```

profile of v0, /device:TPU:0, one launch (start us, length us, event | category | flops | bytes accessed | tf_op | source)
XLA Modules:
  0.0 289.7 jit_solution(6222700549356190898)
XLA Ops:
  8.0 0.0 copy-start
  8.0 0.0 copy-start.1
  8.0 0.0 reduce-scatter.9.cloned.1.call-start
  8.1 0.8 broadcast_multiply_fusion.1
  8.9 0.1 iota_compare_fusion
  9.0 2.0 fusion.12
  11.0 3.4 %convolution_convert_fusion = bf16[16,80,3,3,64]{1,4,3,2,0:T(8,128)(2,1)} fusion(bf16[16,80,768]{2,1,0:T(8,128)(2,1)S(1)} %copy-done.1, f32[768]{0:T(1024)S(1)} %copy-done.9, f32[16,80]{1,0:T(8,128)S(1)} %add_rsqrt_fusion, bf16[768,3,3,64]{0,3,2,1:T(8,128)(2,1)S(1)} %copy-done), kind=kOutput, calls=%fused_computation.20 | convolution fusion | flops 1137131520 | bytes 4333568 | tf_op jit(solution)/shard_map/bsd,dchk->bschk/dot_general | solution.py:14
  14.5 3.6 %fusion.51 = (f32[16,3,80]{2,1,0:T(4,128)S(1)}, f32[16,3,80,80]{2,3,1,0:T(8,128)}) fusion(pred[16,80]{1,0:T(8,128)(4,1)S(1)} %iota_compare_fusion, bf16[16,80,3,3,64]{1,4,3,2,0:T(8,128)(2,1)} %convolution_convert_fusion), kind=kOutput, calls=%fused_computation.69 | convolution fusion | flops 40243280 | bytes 2818304 | tf_op jit(solution)/shard_map/sub | solution.py:25
  18.1 2.3 fusion.27
  20.4 0.0 copy-start.5
  20.4 0.9 copy-done.5
  21.4 0.9 fusion.31
  22.3 1.5 copy.40
  23.8 2.7 reshape.73
  26.5 0.0 reduce-scatter.9.cloned.1.call-update
  26.5 0.0 reduce-scatter.7.cloned.1.call-start
  26.6 0.0 copy-done.8
  26.6 0.0 copy-start.3
  26.6 2.6 fusion.24
  29.2 0.6 fusion.30
  29.9 1.0 copy-done.4
  30.9 0.6 multiply_reduce_fusion
  31.5 0.5 multiply_convert_fusion
  32.0 0.4 fusion.28
  32.4 0.6 fusion.29
  33.0 0.0 copy-done.11
  33.0 3.0 %fusion.14 = f32[768,3,3,64,1]{0,3,2,4,1:T(8,128)} fusion(bf16[16,80,768]{2,1,0:T(8,128)(2,1)S(1)} %copy-done.1, f32[768]{0:T(1024)S(1)} %copy-done.9, f32[16,80]{1,0:T(8,128)S(1)} %add_rsqrt_fusion, bf16[16,80,1,3,64]{1,4,3,0,2:T(8,128)(2,1)S(1)} %fusion.30, bf16[16,80,1,3,64]{1,4,3,0,2:T(8,128)(2,1)S(1)} %fusion.29, ...), kind=kOutput, calls=%fused_computation.21 | convolution fusion | flops 1140817920 | bytes 5218304 | tf_op jit(solution)/shard_map/bsd,bschk->dchk/dot_general | solution.py:58
  36.0 2.8 copy.42
  38.8 0.0 reduce-scatter.7.cloned.1.call-update
  38.9 0.0 all-reduce.6.cloned.1.call-start
  38.9 5.4 %convolution_bitcast_fusion = f32[16,80,768]{2,1,0:T(8,128)} fusion(bf16[16,80,1,3,64]{1,4,3,0,2:T(8,128)(2,1)} %copy-done.11, bf16[16,80,1,3,64]{1,4,3,0,2:T(8,128)(2,1)} %copy-done.7, bf16[16,80,1,3,64]{1,4,3,0,2:T(8,128)(2,1)} %copy-done.6, bf16[768,3,3,64]{0,3,2,1:T(8,128)(2,1)S(1)} %copy-done), kind=kOutput, calls=%fused_computation.19 | convolution fusion | flops 1133936640 | bytes 6291456 | tf_op jit(solution)/shard_map/bschk,dchk->bsd/dot_general | solution.py:59
  44.3 0.0 all-reduce.6.cloned.1.call-update
  44.3 0.0 copy-start.10
  44.3 0.2 all-reduce.4.cloned.1.call-start
  44.6 3.2 %bitcast_convert_fusion = bf16[16,80,768]{2,1,0:T(8,128)(2,1)} fusion(bf16[16,80,3,64]{1,3,2,0:T(8,128)(2,1)} %copy-done.5, bf16[3,64,768]{2,1,0:T(8,128)(2,1)S(1)} %copy-done.8), kind=kOutput, calls=%fused_computation.17 | convolution fusion | flops 378470400 | bytes 2752512 | tf_op jit(solution)/shard_map/zagm,gms->zas/dot_general | solution.py:31
  47.8 0.0 all-reduce.4.cloned.1.call-update
  47.8 0.6 dynamic-slice
  49.1 15.3 %reduce-scatter.9.cloned.1.call-done = f32[96,192]{1,0:T(8,128)} async-done(((f32[768,192]{1,0:T(8,128)}), f32[96,192]{1,0:T(8,128)}) %reduce-scatter.9.cloned.1.call-update) | async-done | bytes 73744
  64.3 1.0 reshape.74
  65.4 0.8 copy.41
  66.1 42.4 %reduce-scatter.7.cloned.1.call-done = f32[96,576]{1,0:T(8,128)} async-done(((f32[768,576]{1,0:T(8,128)}), f32[96,576]{1,0:T(8,128)}) %reduce-scatter.7.cloned.1.call-update) | async-done | bytes 221200
  108.5 1.8 copy.43
  110.3 83.2 %all-reduce.6.cloned.1.call-done = f32[16,80,768]{2,1,0:T(8,128)} async-done(((f32[16,80,768]{2,1,0:T(8,128)}), f32[16,80,768]{2,1,0:T(8,128)}) %all-reduce.6.cloned.1.call-update) | async-done | bytes 3932176 | tf_op jit(solution)/shard_map/psum | solution.py:63
  193.4 3.2 %fusion.11 = (f32[768]{0:T(1024)S(1)}, f32[16,80]{1,0:T(8,128)S(1)}) fusion(f32[16,80,768]{2,1,0:T(8,128)} %all-reduce.6.cloned.1.call-done, bf16[16,80,768]{2,1,0:T(8,128)(2,1)S(1)} %copy-done.1, f32[16,80]{1,0:T(8,128)S(1)} %add_rsqrt_fusion, f32[768]{0:T(1024)S(1)} %copy-done.9), kind=kLoop, calls=%fused_computation.14 | loop fusion | flops 6879232 | bytes 5914624 | tf_op jit(solution)/shard_map/reduce_sum | solution.py:64
  196.7 13.8 %all-reduce = f32[768]{0:T(1024)S(1)} all-reduce(f32[768]{0:T(1024)S(1)} %get-tuple-element.5), channel_id=4, replica_groups=mesh['dp'=8,'mp'=4] {'dp'}, use_global_device_ids=true, to_apply=%region_10.11.clone | all-reduce | flops 768 | bytes 6144
  210.5 0.6 dynamic-slice.1
  211.1 65.9 %all-reduce.4.cloned.1.call-done = bf16[16,80,768]{2,1,0:T(8,128)(2,1)} async-done(((bf16[16,80,768]{2,1,0:T(8,128)(2,1)}), bf16[16,80,768]{2,1,0:T(8,128)(2,1)}) %all-reduce.4.cloned.1.call-update) | async-done | bytes 1966096 | tf_op jit(solution)/shard_map/psum | solution.py:34
  277.0 5.3 %fusion.10 = (bf16[16,80,768]{2,1,0:T(8,128)(2,1)}, bf16[16,80,768]{2,1,0:T(8,128)(2,1)}) fusion(bf16[16,80,768]{2,1,0:T(8,128)(2,1)S(1)} %copy-done.1, f32[16,80,768]{2,1,0:T(8,128)} %all-reduce.6.cloned.1.call-done, f32[16,80]{1,0:T(8,128)S(1)} %broadcast_multiply_fusion, f32[768]{0:T(1024)S(1)} %copy-done.9, f32[16,80]{1,0:T(8,128)S(1)} %add_rsqrt_fusion, ...), kind=kLoop, calls=%fused_computation.13 | loop fusion | flops 12779520 | bytes 13777152 | tf_op jit(solution)/shard_map/convert_element_type | solution.py:67
  (17 shorter events, 0.0 us)
Async XLA Ops:
  8.0 3.0 %copy-start = (bf16[768,3,3,64]{0,3,2,1:T(8,128)(2,1)S(1)}, bf16[768,3,3,64]{0,3,2,1:T(8,128)(2,1)}, u32[]{:S(2)}) copy-start(bf16[768,3,3,64]{0,3,2,1:T(8,128)(2,1)} %param.9) | copy-start | bytes 2654212
  8.0 3.0 %copy-start.1 = (bf16[16,80,768]{2,1,0:T(8,128)(2,1)S(1)}, bf16[16,80,768]{2,1,0:T(8,128)(2,1)}, u32[]{:S(2)}) copy-start(bf16[16,80,768]{2,1,0:T(8,128)(2,1)} %param.6) | copy-start | bytes 5898244
  8.0 3.0 %copy-start.9 = (f32[768]{0:T(1024)S(1)}, f32[768]{0:T(1024)}, u32[]{:S(2)}) copy-start(f32[768]{0:T(1024)} %param.8) | copy-start | bytes 9220
  8.0 56.3 %reduce-scatter.9.cloned.1.call-start = ((), (), s32[]{:S(2)}) async-start(), calls=%async_computation.5 | async-start | bytes 884736
  18.1 3.3 %copy-start.2 = (bf16[16,80,768]{2,1,0:T(8,128)(2,1)S(1)}, bf16[16,80,768]{2,1,0:T(8,128)(2,1)}, u32[]{:S(2)}) copy-start(bf16[16,80,768]{2,1,0:T(8,128)(2,1)} %param.11) | copy-start | bytes 5898244
  20.4 0.9 copy-start.5
  23.8 2.8 copy-start.8
  26.5 82.0 %reduce-scatter.7.cloned.1.call-start = ((), (), s32[]{:S(2)}) async-start(), calls=%async_computation.4 | async-start | bytes 2211840
  26.6 2.6 copy-start.3
  29.2 1.7 copy-start.4
  30.9 2.1 copy-start.11
  32.4 3.6 %copy-start.6 = (bf16[16,80,1,3,64]{1,4,3,0,2:T(8,128)(2,1)}, bf16[16,80,1,3,64]{1,4,3,0,2:T(8,128)(2,1)S(1)}, u32[]{:S(2)}) copy-start(bf16[16,80,1,3,64]{1,4,3,0,2:T(8,128)(2,1)S(1)} %fusion.28) | copy-start | bytes 1474564
  33.0 3.0 %copy-start.7 = (bf16[16,80,1,3,64]{1,4,3,0,2:T(8,128)(2,1)}, bf16[16,80,1,3,64]{1,4,3,0,2:T(8,128)(2,1)S(1)}, u32[]{:S(2)}) copy-start(bf16[16,80,1,3,64]{1,4,3,0,2:T(8,128)(2,1)S(1)} %fusion.29) | copy-start | bytes 1474564
  38.9 154.6 %all-reduce.6.cloned.1.call-start = ((), (), s32[]{:S(2)}) async-start(), calls=%async_computation.3 | async-start | bytes 7864320 | tf_op jit(solution)/shard_map/psum | solution.py:63
  44.3 3.5 %copy-start.10 = (u32[32]{0:T(128)S(1)}, u32[32]{0:T(128)}, u32[]{:S(2)}) copy-start(u32[32]{0:T(128)} %constant.20) | copy-start | bytes 388
  44.3 232.6 %all-reduce.4.cloned.1.call-start = ((), (), s32[]{:S(2)}) async-start(), calls=%async_computation.2 | async-start | bytes 3932160 | tf_op jit(solution)/shard_map/psum | solution.py:34
Sparse Core Ops, SparseCore 0:
  26.6 37.6 reduce-scatter.8
  68.3 40.1 reduce-scatter.6
Sparse Core Ops, SparseCore 1:
  44.4 149.0 all-reduce.5
  196.3 80.6 all-reduce.3
where the time goes:
time: 290 us
  waiting for transfers between devices  207 us (71%)
  matrix products  26.7 us (9%)
  between operations  16.3 us (6%)
  local copies, waits for them, and re-layouts  13.8 us (5%)
  blocking collectives  13.8 us (5%)
  other arithmetic  11.9 us (4%)
    psum x1, waiting for transfers between devices, body(): grad_normed = lax.psum(partial_normed, 'mp')  83.2 us
    psum x1, waiting for transfers between devices, body(): lax.psum(partial_mix.astype(jnp.bfloat16), 'mp').astype(jnp.float32)  65.9 us
    unnamed x6, waiting for transfers between devices  57.7 us
    unnamed x1, blocking collectives  13.8 us
    unnamed x32, local copies, waits for them, and re-layouts  13.8 us
  transfers between devices with their start and end apart: 4, of which 4 were waited for; matrix products, arithmetic and copies ran while one was open for 10% of the time, Pallas kernels for 0%

commit v1 on v0

--- a/solution.py
+++ b/solution.py
@@ -31,7 +31,9 @@
     partial_mix = jnp.einsum(
         "zagm,gms->zas", attended_context, output_weight, preferred_element_type=jnp.float32
     )
-    mixed_total_sum = lax.psum(partial_mix.astype(jnp.bfloat16), "mp").astype(jnp.float32)
+    mixed_total_sum = jnp.sum(
+        lax.all_gather(partial_mix.astype(jnp.bfloat16), axis_name="mp"), axis=0
+    ).astype(jnp.float32)
     attended = (wide_states + mixed_total_sum).astype(jnp.bfloat16)
     masked_cotangent = jnp.where(keep_mask[:, :, None], cotangent, jnp.zeros_like(cotangent))
     local_output = jnp.einsum(

time: 290 us -> 353 us (1.22)
  waiting for transfers between devices: 207 us -> 266 us
  other arithmetic: 11.9 us -> 17.5 us
    all_gather x0 -> x1, waiting for transfers between devices: none -> 125 us  [body(): lax.all_gather(partial_mix.astype(jnp.bfloat16), axis_name='mp')]
    psum x1 -> x0, waiting for transfers between devices: 65.9 us -> none  [body(): lax.psum(partial_mix.astype(jnp.bfloat16), 'mp').astype(jnp.float32)]
    reduce_sum x0 -> x1, other arithmetic: none -> 6.21 us  [body(): jnp.sum(lax.all_gather(partial_mix.astype(jnp.bfloat16), axis_name='mp'),...]
    unnamed x32 -> x34, local copies, waits for them, and re-layouts: 13.8 us -> 13 us
  transfers between devices with their start and end apart: 4 -> 4, of which waited for: 4 -> 4; matrix products, arithmetic and copies ran while one was open for 10% -> 8% of each run, Pallas kernels for 0% -> 0%
where the time goes in v1:
time: 353 us
  waiting for transfers between devices  266 us (75%)
  matrix products  26.8 us (8%)
  other arithmetic  17.5 us (5%)
  between operations  16.3 us (5%)
  blocking collectives  13.4 us (4%)
  local copies, waits for them, and re-layouts  13 us (4%)
    all_gather x1, waiting for transfers between devices, body(): lax.all_gather(partial_mix.astype(jnp.bfloat16), axis_name='mp')  125 us
    psum x1, waiting for transfers between devices, body(): grad_normed = lax.psum(partial_normed, 'mp')  82.5 us
    unnamed x6, waiting for transfers between devices  58.4 us
    unnamed x1, blocking collectives  13.4 us
    unnamed x34, local copies, waits for them, and re-layouts  13 us
  transfers between devices with their start and end apart: 4, of which 4 were waited for; matrix products, arithmetic and copies ran while one was open for 8% of the time, Pallas kernels for 0%

profile of v1, /device:TPU:0, one launch (start us, length us, event | category | flops | bytes accessed | tf_op | source)
XLA Modules:
  0.0 353.0 jit_solution(12529718057468380364)
XLA Ops:
  8.0 0.0 copy-start
  8.0 0.0 copy-start.1
  8.0 0.0 reduce-scatter.9.cloned.1.call-start
  8.1 2.2 fusion.12
  10.3 0.1 iota_compare_fusion
  10.4 0.1 copy-done.1
  10.4 3.4 convolution_convert_fusion
  13.9 3.6 %fusion.51 = (f32[16,3,80]{2,1,0:T(4,128)S(1)}, f32[16,3,80,80]{2,3,1,0:T(8,128)}) fusion(pred[16,80]{1,0:T(8,128)(4,1)S(1)} %iota_compare_fusion, bf16[16,80,3,3,64]{1,4,3,2,0:T(8,128)(2,1)} %convolution_convert_fusion), kind=kOutput, calls=%fused_computation.69 | convolution fusion | flops 40243280 | bytes 2818304 | tf_op jit(solution)/shard_map/sub | solution.py:25
  17.5 2.3 fusion.27
  19.8 0.9 copy-done.5
  20.7 0.9 fusion.31
  21.6 1.5 copy.40
  23.1 2.7 reshape.74
  25.8 0.0 reduce-scatter.9.cloned.1.call-update
  25.9 0.0 reduce-scatter.7.cloned.1.call-start
  25.9 0.0 copy-start.3
  26.0 2.6 fusion.24
  28.6 0.2 copy-done.4
  28.8 0.6 multiply_reduce_fusion
  29.4 0.6 fusion.30
  30.1 0.0 copy-start.12
  30.1 0.5 multiply_convert_fusion
  30.5 0.4 fusion.28
  31.0 0.6 fusion.29
  31.6 0.0 copy-done.12
  31.6 3.0 fusion.14
  34.6 2.8 copy.42
  37.4 0.0 reduce-scatter.7.cloned.1.call-update
  37.4 0.0 all-reduce.3.cloned.1.call-start
  37.5 5.5 %convolution_bitcast_fusion = f32[16,80,768]{2,1,0:T(8,128)} fusion(bf16[16,80,1,3,64]{1,4,3,0,2:T(8,128)(2,1)} %copy-done.12, bf16[16,80,1,3,64]{1,4,3,0,2:T(8,128)(2,1)} %copy-done.7, bf16[16,80,1,3,64]{1,4,3,0,2:T(8,128)(2,1)} %copy-done.6, bf16[768,3,3,64]{0,3,2,1:T(8,128)(2,1)S(1)} %copy-done), kind=kOutput, calls=%fused_computation.19 | convolution fusion | flops 1133936640 | bytes 6291456 | tf_op jit(solution)/shard_map/bschk,dchk->bsd/dot_general | solution.py:61
  43.0 0.0 all-reduce.3.cloned.1.call-update
  43.0 0.0 copy-start.11
  43.0 0.2 all-gather.3.cloned.1.call-start
  43.2 3.2 bitcast_convert_fusion
  46.4 0.0 all-gather.3.cloned.1.call-update
  46.5 0.6 dynamic-slice
  47.7 16.0 %reduce-scatter.9.cloned.1.call-done = f32[96,192]{1,0:T(8,128)} async-done(((f32[768,192]{1,0:T(8,128)}), f32[96,192]{1,0:T(8,128)}) %reduce-scatter.9.cloned.1.call-update) | async-done | bytes 73744
  63.7 1.0 reshape.75
  64.7 0.8 copy.41
  65.4 42.4 %reduce-scatter.7.cloned.1.call-done = f32[96,576]{1,0:T(8,128)} async-done(((f32[768,576]{1,0:T(8,128)}), f32[96,576]{1,0:T(8,128)}) %reduce-scatter.7.cloned.1.call-update) | async-done | bytes 221200
  107.8 1.8 copy.43
  109.7 82.5 %all-reduce.3.cloned.1.call-done = f32[16,80,768]{2,1,0:T(8,128)} async-done(((f32[16,80,768]{2,1,0:T(8,128)}), f32[16,80,768]{2,1,0:T(8,128)}) %all-reduce.3.cloned.1.call-update) | async-done | bytes 3932176 | tf_op jit(solution)/shard_map/psum | solution.py:65
  192.1 3.2 fusion.11
  195.4 13.4 %all-reduce = f32[768]{0:T(1024)S(1)} all-reduce(f32[768]{0:T(1024)S(1)} %get-tuple-element.5), channel_id=5, replica_groups=mesh['dp'=8,'mp'=4] {'dp'}, use_global_device_ids=true, to_apply=%region_10.11.clone | all-reduce | flops 768 | bytes 6144
  208.8 0.6 dynamic-slice.1
  209.4 124.7 %all-gather.3.cloned.1.call-done = bf16[64,80,768]{2,1,0:T(8,128)(2,1)} async-done(((bf16[16,80,768]{2,1,0:T(8,128)(2,1)}), bf16[64,80,768]{2,1,0:T(8,128)(2,1)}) %all-gather.3.cloned.1.call-update) | async-done | bytes 7864336 | tf_op jit(solution)/shard_map/all_gather | solution.py:35
  334.1 6.2 %reduce_sum.59 = bf16[16,80,768]{2,1,0:T(8,128)(2,1)} reduce(bf16[4,16,80,768]{3,2,1,0:T(8,128)(2,1)} %bitcast.105, bf16[]{:T(256)} %constant.16.clone.1), dimensions={0}, to_apply=%region_3.4 | reduce | flops 2949120 | bytes 9830402 | tf_op jit(solution)/shard_map/reduce_sum | solution.py:34
  340.3 5.3 %fusion.10 = (bf16[16,80,768]{2,1,0:T(8,128)(2,1)}, bf16[16,80,768]{2,1,0:T(8,128)(2,1)}) fusion(bf16[16,80,768]{2,1,0:T(8,128)(2,1)S(1)} %copy-done.1, f32[16,80,768]{2,1,0:T(8,128)} %all-reduce.3.cloned.1.call-done, f32[16,80]{1,0:T(8,128)S(1)} %broadcast_multiply_fusion, f32[768]{0:T(1024)S(1)} %copy-done.9, f32[16,80]{1,0:T(8,128)S(1)} %add_rsqrt_fusion, ...), kind=kLoop, calls=%fused_computation.13 | loop fusion | flops 12779520 | bytes 13777152 | tf_op jit(solution)/shard_map/convert_element_type | solution.py:69
  (20 shorter events, 0.0 us)
Async XLA Ops:
  8.0 2.4 copy-start
  8.0 2.4 copy-start.1
  8.0 2.3 copy-start.10
  8.0 2.4 copy-start.9
  8.0 55.6 %reduce-scatter.9.cloned.1.call-start = ((), (), s32[]{:S(2)}) async-start(), calls=%async_computation.5 | async-start | bytes 884736
  17.4 3.3 copy-start.2
  19.8 0.9 copy-start.5
  23.1 2.8 copy-start.8
  25.9 82.0 %reduce-scatter.7.cloned.1.call-start = ((), (), s32[]{:S(2)}) async-start(), calls=%async_computation.4 | async-start | bytes 2211840
  25.9 2.6 copy-start.3
  25.9 2.8 copy-start.4
  30.1 1.5 copy-start.12
  30.9 3.6 %copy-start.6 = (bf16[16,80,1,3,64]{1,4,3,0,2:T(8,128)(2,1)}, bf16[16,80,1,3,64]{1,4,3,0,2:T(8,128)(2,1)S(1)}, u32[]{:S(2)}) copy-start(bf16[16,80,1,3,64]{1,4,3,0,2:T(8,128)(2,1)S(1)} %fusion.28) | copy-start | bytes 1474564
  31.6 3.0 copy-start.7
  37.4 154.7 %all-reduce.3.cloned.1.call-start = ((), (), s32[]{:S(2)}) async-start(), calls=%async_computation.2 | async-start | bytes 7864320 | tf_op jit(solution)/shard_map/psum | solution.py:65
  43.0 3.5 copy-start.11
  43.0 291.1 %all-gather.3.cloned.1.call-start = ((), (), s32[]{:S(2)}) async-start(), calls=%async_computation.3 | async-start | bytes 9830400 | tf_op jit(solution)/shard_map/all_gather | solution.py:35
Sparse Core Ops, SparseCore 0:
  26.0 37.6 reduce-scatter.8
  67.7 40.1 reduce-scatter.6
Sparse Core Ops, SparseCore 1:
  43.1 149.0 all-reduce.2
  194.2 139.9 all-gather.2
